TPU v7x, 256 devices: a whole 4x4x8 slice. The times are simulated.
256 devices in a mesh: dp: 8 (over z_lo, core), ep: 32 (over x, y, z_hi).
Axes of the slice: x: 4, y: 4, z: 8 (z_hi: 2, z_lo: 4; z = z_hi * 4 + z_lo), core: 2. Of those that a mesh axis runs over, the one named last changes fastest.
Arguments:
- tokens: bfloat16 [32768, 7168], P(('dp', 'ep')), may hold values from -6 to 6
- out_grad: bfloat16 [32768, 7168], P(('dp', 'ep')), may hold values from -3 to 3
- expert_ids: int32 [32768, 8], P(('dp', 'ep')), may hold values from 0 to 255, as said below
- route_weights: bfloat16 [32768, 8], P(('dp', 'ep')), may hold values from 0.099609375 to 1
- gate_matrix: bfloat16 [7168, 8192], P('dp', 'ep'), may hold values from -0.0625 to 0.0625
- up_matrix: bfloat16 [7168, 8192], P('dp', 'ep'), may hold values from -0.0625 to 0.0625
- down_matrix: bfloat16 [7168, 8192], P('dp', 'ep'), may hold values from -0.125 to 0.125
Outputs:
- input_gradient: bfloat16 [32768, 7168], P(('dp', 'ep'))
- route_gradient: float32 [32768, 8], P(('dp', 'ep'))
- gate_gradient: bfloat16 [7168, 8192], P('dp', 'ep')
- up_gradient: bfloat16 [7168, 8192], P('dp', 'ep')
- down_gradient: bfloat16 [7168, 8192], P('dp', 'ep')
Inputs may be any that keep to these rules, and one draw needn't show every extreme that they name: `expert_ids`: each row names 8 different ids, 2 in each of 4 groups of 32 consecutive ids. In each aligned block of 4096 rows, one id that is a multiple of 64 is named by 8 or more rows of every aligned block of 128 rows inside it.
All inputs are finite; a program needn't handle non-finite values.
Results may differ from a plain program's by a relative error of at most 0.014.
Values may be sent and summed in bfloat16 or wider, within the bound.
No kernel may reach another device: no remote copies, remote signals or barrier semaphores. Data moves between devices by JAX's collectives and lax.ppermute only.
A program may use at most 128 MiB of HBM per device.

v0:
```python
import math
import jax
import jax.numpy as jnp
from jax import lax
from jax.sharding import PartitionSpec as P

ROUTED = 256
TOPK = 8
SLICES = 8
CAP = 8


def in_one_piece(arrays, axis, split_dim, concat_dim, along):
    widths = [math.prod(a.shape[along:]) for a in arrays]
    both = jnp.concatenate(
        [a.reshape(*a.shape[:along], w) for a, w in zip(arrays, widths)], axis=along
    )
    filled = lax.all_to_all(both, axis, split_axis=split_dim, concat_axis=concat_dim, tiled=True)
    tiles = jnp.split(filled, [sum(widths[:k]) for k in range(1, len(widths))], axis=along)
    return tuple(
        (b.reshape(*filled.shape[:along], *a.shape[along:]) for a, b in zip(arrays, tiles))
    )


def hidden_terms(gate_pre, up_pre, projected, gate_rows):
    sigmoid = jax.nn.sigmoid(gate_pre)
    swished = gate_pre * sigmoid
    hidden = lax.optimization_barrier((swished * up_pre).astype(jnp.bfloat16)).astype(jnp.float32)
    route_part = jnp.sum(hidden * projected, axis=1).astype(jnp.bfloat16)
    scaling = gate_rows.astype(jnp.float32)[:, None]
    grad_hidden = scaling * projected
    gate_delta = grad_hidden * up_pre * sigmoid * (1.0 + gate_pre * (1.0 - sigmoid))
    up_delta = grad_hidden * swished
    deltas = jnp.concatenate([gate_delta, up_delta], axis=1).astype(jnp.bfloat16)
    scaled = (scaling * hidden).astype(jnp.bfloat16)
    return (deltas, scaled, route_part)


def body(tokens, out_grad, expert_ids, route_weights, gate_matrix, up_matrix, down_matrix):
    senders = lax.axis_size("ep")
    experts = senders // SLICES
    stride = ROUTED // experts
    tok_rows = tokens.shape[0]
    width = tokens.shape[1]
    hid_width = gate_matrix.shape[1]
    flat_ids = expert_ids.reshape(tok_rows * TOPK)
    window = flat_ids % stride == 0
    expert = jnp.where(window, flat_ids // stride, experts)
    column = jnp.arange(experts, dtype=jnp.int32)
    onehot = (expert[:, None] == column[None, :]).astype(jnp.int32)
    earlier = jnp.cumsum(onehot, axis=0) - onehot
    slot_index = jnp.sum(earlier * onehot, axis=1)
    kept_entry = window & (slot_index < CAP)
    places = jnp.arange(experts * CAP, dtype=jnp.int32)
    assign = kept_entry[:, None] & ((expert * CAP + slot_index)[:, None] == places[None, :])
    assign = assign.astype(jnp.float32).reshape(tok_rows, TOPK, experts * CAP)
    select = jnp.sum(assign, axis=1).astype(jnp.bfloat16)
    slot_in = jnp.einsum("ts,td->sd", select, tokens, preferred_element_type=jnp.float32).astype(
        jnp.bfloat16
    )
    slot_grad = jnp.einsum(
        "ts,td->sd", select, out_grad, preferred_element_type=jnp.float32
    ).astype(jnp.bfloat16)
    slot_gate = jnp.einsum("tks,tk->s", assign, route_weights.astype(jnp.float32)).astype(
        jnp.bfloat16
    )
    send_in = jnp.repeat(slot_in.reshape(experts, CAP, width), SLICES, axis=0)
    send_grad = jnp.repeat(slot_grad.reshape(experts, CAP, width), SLICES, axis=0)
    send_gate = jnp.repeat(slot_gate.reshape(experts, CAP), SLICES, axis=0)
    rows_in, rows_grad, rows_gate = in_one_piece((send_in, send_grad, send_gate), "ep", 0, 0, 2)
    total_rows = senders * CAP
    rows_in = rows_in.reshape(total_rows, width)
    rows_grad = rows_grad.reshape(total_rows, width)
    rows_gate = rows_gate.reshape(total_rows)
    stacked = jnp.concatenate([gate_matrix, up_matrix], axis=1)
    full_pair, full_down = (
        lax.all_gather(stacked, "dp", axis=0, tiled=True),
        lax.all_gather(down_matrix, "dp", axis=0, tiled=True),
    )
    gate_up = jnp.dot(rows_in, full_pair, preferred_element_type=jnp.float32)
    projected = jnp.dot(rows_grad, full_down, preferred_element_type=jnp.float32)
    deltas, scaled, route_part = hidden_terms(
        gate_up[:, :hid_width], gate_up[:, hid_width:], projected, rows_gate
    )
    partial_value = jnp.einsum(
        "rh,dh->rd", deltas, full_pair, preferred_element_type=jnp.float32
    ).astype(jnp.bfloat16)
    left = jnp.einsum("rd,rh->dh", rows_in, deltas, preferred_element_type=jnp.float32)
    right = jnp.einsum("rd,rh->dh", rows_grad, scaled, preferred_element_type=jnp.float32)
    summed = lax.psum_scatter(
        jnp.concatenate([left, right], axis=1).astype(jnp.bfloat16),
        "dp",
        scatter_dimension=0,
        tiled=True,
    ).astype(jnp.float32)
    back_in, back_route = in_one_piece(
        (partial_value.reshape(senders, CAP, width), route_part.reshape(senders, CAP)),
        "ep",
        0,
        0,
        2,
    )
    slot_sums = jnp.sum(
        back_in.reshape(experts, SLICES, CAP, width).astype(jnp.float32), axis=1
    ).reshape(experts * CAP, width)
    route_sums = jnp.sum(
        back_route.reshape(experts, SLICES, CAP).astype(jnp.float32), axis=1
    ).reshape(experts * CAP)
    input_gradient = jnp.dot(select.astype(jnp.float32), slot_sums).astype(jnp.bfloat16)
    route_gradient = jnp.einsum("tks,s->tk", assign, route_sums)
    gate_gradient = summed[:, :hid_width].astype(jnp.bfloat16)
    up_gradient = summed[:, hid_width : 2 * hid_width].astype(jnp.bfloat16)
    down_gradient = summed[:, 2 * hid_width :].astype(jnp.bfloat16)
    return (input_gradient, route_gradient, gate_gradient, up_gradient, down_gradient)


def solution(mesh):
    return jax.shard_map(
        body,
        mesh=mesh,
        in_specs=(
            P(("dp", "ep"), None),
            P(("dp", "ep"), None),
            P(("dp", "ep"), None),
            P(("dp", "ep"), None),
            P("dp", "ep"),
            P("dp", "ep"),
            P("dp", "ep"),
        ),
        out_specs=(
            P(("dp", "ep"), None),
            P(("dp", "ep"), None),
            P("dp", "ep"),
            P("dp", "ep"),
            P("dp", "ep"),
        ),
        check_vma=False,
    )
```

profile of v0, /device:TPU:2, one launch (start us, length us, event | category | flops | bytes accessed | tf_op | source)
XLA Modules:
  0.0 537.9 jit_solution(14116264508713704503)
XLA Ops:
  7.2 2.3 pad_maximum_fusion.3
  9.5 0.8 copy.124
  10.5 1.1 reduce-window.6
  13.7 0.8 fusion.5
  15.5 1.9 fusion.1
  18.2 3.5 pad_maximum_fusion.1
  21.7 14.3 %all-to-all-start = ((bf16[32,8,14337]{2,1,0:T(8,128)(2,1)}), bf16[32,8,14337]{2,1,0:T(8,128)(2,1)}, u32[]{:S(2)}, u32[]{:S(2)}) async-start(bf16[32,8,14337]{2,1,0:T(8,128)(2,1)} %pad_maximum_fusion.1), calls=%async_computation | async-start | bytes 14811136 | tf_op jit(solution)/shard_map/all_to_all | solution.py:18
  37.0 225.5 %all-to-all-done = bf16[32,8,14337]{2,1,0:T(8,128)(2,1)} async-done(((bf16[32,8,14337]{2,1,0:T(8,128)(2,1)}), bf16[32,8,14337]{2,1,0:T(8,128)(2,1)}, u32[]{:S(2)}, u32[]{:S(2)}) %all-to-all-start) | async-done | bytes 7340576 | tf_op jit(solution)/shard_map/all_to_all | solution.py:18
  262.5 0.9 convert_reduce_fusion.1
  263.6 7.3 %fusion.4 = f32[256,512]{0,1:T(8,128)S(1)} fusion(bf16[7168,512]{1,0:T(8,128)(2,1)} %all-gather.5.cloned.1.call-done, bf16[32,8,14337]{2,1,0:T(8,128)(2,1)} %all-to-all-done), kind=kOutput, calls=%fused_computation.16 | convolution fusion | flops 1879048192 | bytes 11534336 | tf_op jit(solution)/shard_map/dot_general | solution.py:80
  270.8 22.5 %all-gather.3.cloned.1.call-done = bf16[7168,256]{1,0:T(8,128)(2,1)} async-done(((bf16[896,256]{1,0:T(8,128)(2,1)}), bf16[7168,256]{1,0:T(8,128)(2,1)}) %all-gather.3.cloned.1.call-update) | async-done | bytes 3670032 | tf_op jit(solution)/shard_map/all_gather | solution.py:78
  293.3 4.7 multiply_convert_fusion.2
  298.0 3.2 convolution_convert_fusion.1
  301.2 4.1 convolution_convert_fusion
  305.3 7.8 %pad_maximum_fusion = bf16[7168,768]{0,1:T(8,128)(2,1)} fusion(bf16[7168,256]{0,1:T(8,128)(2,1)S(1)} %convolution_convert_fusion.1, bf16[7168,512]{0,1:T(8,128)(2,1)S(1)} %convolution_convert_fusion), kind=kLoop, calls=%fused_computation | loop fusion | flops 22020096 | bytes 22020096 | tf_op jit(solution)/shard_map/concatenate | solution.py:91
  313.1 14.7 %copy.141 = bf16[7168,768]{1,0:T(8,128)(2,1)} copy(bf16[7168,768]{0,1:T(8,128)(2,1)} %pad_maximum_fusion) | data formatting | bytes 22020096
  328.2 5.2 fusion
  333.7 140.2 %all_to_all.10 = bf16[32,8,7169]{2,1,0:T(8,128)(2,1)S(1)} all-to-all(bf16[32,8,7169]{2,1,0:T(8,128)(2,1)S(1)} %pad_maximum_fusion.2), channel_id=1, replica_groups=mesh['dp'=8,'ep'=32] {'ep'}, dimensions={0} | all-to-all | bytes 7341056 | tf_op jit(solution)/shard_map/all_to_all | solution.py:18
  473.9 1.9 copy-done.2
  476.3 0.7 fusion.18
  477.1 2.6 convert_reduce_fusion
  479.7 1.9 convolution_convert_fusion.3
  481.6 47.4 %reduce-scatter.4.cloned.1.call-done = bf16[896,768]{1,0:T(8,128)(2,1)} async-done(((bf16[7168,768]{1,0:T(8,128)(2,1)}), bf16[896,768]{1,0:T(8,128)(2,1)}) %reduce-scatter.4.cloned.1.call-update) | async-done | bytes 1376272
  529.0 2.4 fusion.46
  (44 shorter events, 6.2 us)
Async XLA Ops:
  7.2 8.0 %copy-start = (bf16[128,7168]{1,0:T(8,128)(2,1)S(1)}, bf16[128,7168]{1,0:T(8,128)(2,1)}, u32[]{:S(2)}) copy-start(bf16[128,7168]{1,0:T(8,128)(2,1)} %param.8) | copy-start | bytes 5505028
  7.2 256.4 %all-gather.5.cloned.1.call-start = ((), (), s32[]{:S(2)}) async-start(), calls=%async_computation.4 | async-start | bytes 8257536 | tf_op jit(solution)/shard_map/all_gather | solution.py:77
  21.7 240.7 %all-to-all-start = ((bf16[32,8,14337]{2,1,0:T(8,128)(2,1)}), bf16[32,8,14337]{2,1,0:T(8,128)(2,1)}, u32[]{:S(2)}, u32[]{:S(2)}) async-start(bf16[32,8,14337]{2,1,0:T(8,128)(2,1)} %pad_maximum_fusion.1), calls=%async_computation | async-start | bytes 14811136 | tf_op jit(solution)/shard_map/all_to_all | solution.py:18
  36.0 257.2 %all-gather.3.cloned.1.call-start = ((), (), s32[]{:S(2)}) async-start(), calls=%async_computation.3 | async-start | bytes 4128768 | tf_op jit(solution)/shard_map/all_gather | solution.py:78
  36.8 492.2 %reduce-scatter.4.cloned.1.call-start = ((), (), s32[]{:S(2)}) async-start(), calls=%async_computation.5 | async-start | bytes 12386304
  333.4 198.0 %copy-start.1 = (bf16[128,7168]{1,0:T(8,128)(2,1)S(1)}, bf16[128,7168]{1,0:T(8,128)(2,1)}, u32[]{:S(2)}) copy-start(bf16[128,7168]{1,0:T(8,128)(2,1)} %param.8) | copy-start | bytes 5505028
  473.9 1.9 copy-start.2
Sparse Core Ops, SparseCore 0:
  10.4 200.9 all-gather.4
  213.2 80.0 all-gather.2
  328.0 200.9 reduce-scatter.3
where the time goes:
time: 539 us; the launch traced here: 538 us
  waiting for transfers between devices  296 us (55%)
  blocking collectives  140 us (26%)
  matrix products  30.2 us (6%)
  local copies, waits for them, and re-layouts  22.4 us (4%)
  other arithmetic  20.5 us (4%)
  starting transfers between devices  14.6 us (3%)
  between operations  13.9 us (3%)
    all_to_all x1, waiting for transfers between devices, in_one_piece(): lax.all_to_all(both, axis, split_axis=split_dim, concat_axis=concat_dim,...  225 us
    all_to_all x1, blocking collectives, in_one_piece(): lax.all_to_all(both, axis, split_axis=split_dim, concat_axis=concat_dim,...  140 us
    unnamed x4, waiting for transfers between devices  48.1 us
    all_gather x1, waiting for transfers between devices, body(): lax.all_gather(down_matrix, 'dp', axis=0, tiled=True)  22.5 us
    unnamed x9, local copies, waits for them, and re-layouts  17.6 us
    all_to_all x1, starting transfers between devices, in_one_piece(): lax.all_to_all(both, axis, split_axis=split_dim, concat_axis=concat_dim,...  14.3 us
  transfers between devices with their start and end apart: 4, of which 3 were waited for; matrix products, arithmetic and copies ran while one was open for 6% of the time, Pallas kernels for 0%

commit v1 on v0

--- a/solution.py
+++ b/solution.py
@@ -75,7 +75,9 @@
     stacked = jnp.concatenate([gate_matrix, up_matrix], axis=1)
     full_pair, full_down = (
         lax.all_gather(stacked, "dp", axis=0, tiled=True),
-        lax.all_gather(down_matrix, "dp", axis=0, tiled=True),
+        jnp.concatenate(
+            lax.all_to_all(jnp.stack([down_matrix] * lax.axis_size("dp")), "dp", 0, 0), axis=0
+        ),
     )
     gate_up = jnp.dot(rows_in, full_pair, preferred_element_type=jnp.float32)
     projected = jnp.dot(rows_grad, full_down, preferred_element_type=jnp.float32)

time: 539 us -> 604 us (1.12)
  waiting for transfers between devices: 296 us -> 345 us
  starting transfers between devices: 14.6 us -> 31.8 us
    all_to_all x0 -> x1, waiting for transfers between devices: none -> 74.4 us  [body(): lax.all_to_all(jnp.stack([down_matrix] * lax.axis_size('dp')), 'dp', 0, 0)]
    all_gather x1 -> x0, waiting for transfers between devices: 22.5 us -> none  [body(): lax.all_gather(down_matrix, 'dp', axis=0, tiled=True)]
    all_to_all x0 -> x1, starting transfers between devices: none -> 17.1 us  [body(): lax.all_to_all(jnp.stack([down_matrix] * lax.axis_size('dp')), 'dp', 0, 0)]
    unnamed x4 -> x3, waiting for transfers between devices: 48.1 us -> 47.9 us
    unnamed x9 -> x15, local copies, waits for them, and re-layouts: 17.6 us -> 17.7 us
  transfers between devices with their start and end apart: 4 -> 4, of which waited for: 3 -> 3; matrix products, arithmetic and copies ran while one was open for 6% -> 4% of each run, Pallas kernels for 0% -> 0%
where the time goes in v1:
time: 604 us; the launch traced here: 603 us
  waiting for transfers between devices  345 us (57%)
  blocking collectives  138 us (23%)
  starting transfers between devices  31.8 us (5%)
  matrix products  30.1 us (5%)
  local copies, waits for them, and re-layouts  24.7 us (4%)
  other arithmetic  19.3 us (3%)
  between operations  14.3 us (2%)
    all_to_all x1, waiting for transfers between devices, in_one_piece(): lax.all_to_all(both, axis, split_axis=split_dim, concat_axis=concat_dim,...  222 us
    all_to_all x1, blocking collectives, in_one_piece(): lax.all_to_all(both, axis, split_axis=split_dim, concat_axis=concat_dim,...  138 us
    all_to_all x1, waiting for transfers between devices, body(): lax.all_to_all(jnp.stack([down_matrix] * lax.axis_size('dp')), 'dp', 0, 0)  74.4 us
    unnamed x3, waiting for transfers between devices  47.9 us
    unnamed x15, local copies, waits for them, and re-layouts  17.7 us
    all_to_all x1, starting transfers between devices, body(): lax.all_to_all(jnp.stack([down_matrix] * lax.axis_size('dp')), 'dp', 0, 0)  17.1 us
    all_to_all x1, starting transfers between devices, in_one_piece(): lax.all_to_all(both, axis, split_axis=split_dim, concat_axis=concat_dim,...  14.4 us
  transfers between devices with their start and end apart: 4, of which 3 were waited for; matrix products, arithmetic and copies ran while one was open for 4% of the time, Pallas kernels for 0%

profile of v1, /device:TPU:2, one launch (start us, length us, event | category | flops | bytes accessed | tf_op | source)
XLA Modules:
  0.0 603.0 jit_solution(15357875025925203012)
XLA Ops:
  7.2 0.9 copy.124
  8.3 1.1 reduce-window.6
  13.3 1.9 fusion.1
  16.0 3.5 pad_maximum_fusion.1
  19.5 14.4 %all-to-all-start = ((bf16[32,8,14337]{2,1,0:T(8,128)(2,1)}), bf16[32,8,14337]{2,1,0:T(8,128)(2,1)}, u32[]{:S(2)}, u32[]{:S(2)}) async-start(bf16[32,8,14337]{2,1,0:T(8,128)(2,1)} %pad_maximum_fusion.1), calls=%async_computation | async-start | bytes 14811136 | tf_op jit(solution)/shard_map/all_to_all | solution.py:18
  34.1 1.0 pad_maximum_fusion.3
  35.1 222.3 %all-to-all-done = bf16[32,8,14337]{2,1,0:T(8,128)(2,1)} async-done(((bf16[32,8,14337]{2,1,0:T(8,128)(2,1)}), bf16[32,8,14337]{2,1,0:T(8,128)(2,1)}, u32[]{:S(2)}, u32[]{:S(2)}) %all-to-all-start) | async-done | bytes 7340576 | tf_op jit(solution)/shard_map/all_to_all | solution.py:18
  257.4 2.1 stack.2
  259.5 17.1 %all-to-all-start.1 = ((bf16[8,896,256]{2,1,0:T(8,128)(2,1)}), bf16[8,896,256]{2,1,0:T(8,128)(2,1)}, u32[]{:S(2)}, u32[]{:S(2)}) async-start(bf16[8,896,256]{2,1,0:T(8,128)(2,1)} %stack.2), calls=%async_computation.1 | async-start | bytes 7340032 | tf_op jit(solution)/shard_map/all_to_all | solution.py:79
  276.8 0.9 convert_reduce_fusion.1
  277.9 7.2 %fusion.4 = f32[256,512]{0,1:T(8,128)S(1)} fusion(bf16[7168,512]{1,0:T(8,128)(2,1)} %all-gather.2.cloned.1.call-done, bf16[32,8,14337]{2,1,0:T(8,128)(2,1)} %all-to-all-done), kind=kOutput, calls=%fused_computation.16 | convolution fusion | flops 1879048192 | bytes 11534336 | tf_op jit(solution)/shard_map/dot_general | solution.py:82
  285.1 74.4 %all-to-all-done.1 = bf16[8,896,256]{2,1,0:T(8,128)(2,1)} async-done(((bf16[8,896,256]{2,1,0:T(8,128)(2,1)}), bf16[8,896,256]{2,1,0:T(8,128)(2,1)}, u32[]{:S(2)}, u32[]{:S(2)}) %all-to-all-start.1) | async-done | bytes 3670048 | tf_op jit(solution)/shard_map/all_to_all | solution.py:79
  359.5 4.7 multiply_convert_fusion.2
  364.2 3.2 convolution_convert_fusion.1
  367.4 4.1 convolution_convert_fusion
  371.5 7.8 %pad_maximum_fusion = bf16[7168,768]{0,1:T(8,128)(2,1)} fusion(bf16[7168,256]{0,1:T(8,128)(2,1)S(1)} %convolution_convert_fusion.1, bf16[7168,512]{0,1:T(8,128)(2,1)S(1)} %convolution_convert_fusion), kind=kLoop, calls=%fused_computation | loop fusion | flops 22020096 | bytes 22020096 | tf_op jit(solution)/shard_map/concatenate | solution.py:93
  379.3 14.7 %copy.141 = bf16[7168,768]{1,0:T(8,128)(2,1)} copy(bf16[7168,768]{0,1:T(8,128)(2,1)} %pad_maximum_fusion) | data formatting | bytes 22020096
  394.4 5.2 fusion
  399.8 138.3 %all_to_all.15 = bf16[32,8,7169]{2,1,0:T(8,128)(2,1)S(1)} all-to-all(bf16[32,8,7169]{2,1,0:T(8,128)(2,1)S(1)} %pad_maximum_fusion.2), channel_id=1, replica_groups=mesh['dp'=8,'ep'=32] {'ep'}, dimensions={0} | all-to-all | bytes 7341056 | tf_op jit(solution)/shard_map/all_to_all | solution.py:18
  538.1 1.9 copy-done.2
  541.3 2.7 convert_reduce_fusion
  544.0 1.9 convolution_convert_fusion.3
  545.9 47.9 %reduce-scatter.4.cloned.1.call-done = bf16[896,768]{1,0:T(8,128)(2,1)} async-done(((bf16[7168,768]{1,0:T(8,128)(2,1)}), bf16[896,768]{1,0:T(8,128)(2,1)}) %reduce-scatter.4.cloned.1.call-update) | async-done | bytes 1376272
  593.8 2.4 fusion.46
  (50 shorter events, 7.1 us)
Async XLA Ops:
  7.2 5.8 copy-start
  19.5 14.5 %copy-start.3 = (bf16[896,256]{1,0:T(8,128)(2,1)S(1)}, bf16[896,256]{1,0:T(8,128)(2,1)}, u32[]{:S(2)}) copy-start(bf16[896,256]{1,0:T(8,128)(2,1)} %param.12) | copy-start | bytes 1376260
  19.5 14.5 %copy-start.4 = (bf16[896,256]{1,0:T(8,128)(2,1)S(1)}, bf16[896,256]{1,0:T(8,128)(2,1)}, u32[]{:S(2)}) copy-start(bf16[896,256]{1,0:T(8,128)(2,1)} %param.11) | copy-start | bytes 1376260
  19.5 237.8 %copy-start.5 = (bf16[896,256]{1,0:T(8,128)(2,1)S(1)}, bf16[896,256]{1,0:T(8,128)(2,1)}, u32[]{:S(2)}) copy-start(bf16[896,256]{1,0:T(8,128)(2,1)} %param.13) | copy-start | bytes 1376260
  19.5 237.8 %all-to-all-start = ((bf16[32,8,14337]{2,1,0:T(8,128)(2,1)}), bf16[32,8,14337]{2,1,0:T(8,128)(2,1)}, u32[]{:S(2)}, u32[]{:S(2)}) async-start(bf16[32,8,14337]{2,1,0:T(8,128)(2,1)} %pad_maximum_fusion.1), calls=%async_computation | async-start | bytes 14811136 | tf_op jit(solution)/shard_map/all_to_all | solution.py:18
  34.0 243.9 %all-gather.2.cloned.1.call-start = ((), (), s32[]{:S(2)}) async-start(), calls=%async_computation.4 | async-start | bytes 8257536 | tf_op jit(solution)/shard_map/all_gather | solution.py:77
  259.5 100.0 %all-to-all-start.1 = ((bf16[8,896,256]{2,1,0:T(8,128)(2,1)}), bf16[8,896,256]{2,1,0:T(8,128)(2,1)}, u32[]{:S(2)}, u32[]{:S(2)}) async-start(bf16[8,896,256]{2,1,0:T(8,128)(2,1)} %stack.2), calls=%async_computation.1 | async-start | bytes 7340032 | tf_op jit(solution)/shard_map/all_to_all | solution.py:79
  276.6 317.1 %reduce-scatter.4.cloned.1.call-start = ((), (), s32[]{:S(2)}) async-start(), calls=%async_computation.5 | async-start | bytes 12386304
  399.6 196.6 %copy-start.1 = (bf16[128,7168]{1,0:T(8,128)(2,1)S(1)}, bf16[128,7168]{1,0:T(8,128)(2,1)}, u32[]{:S(2)}) copy-start(bf16[128,7168]{1,0:T(8,128)(2,1)} %param.8) | copy-start | bytes 5505028
  538.1 1.9 copy-start.2
Sparse Core Ops, SparseCore 0:
  37.2 218.7 all-gather.1
  394.2 199.5 reduce-scatter.3
